TPU v7x, 128 devices: a 2x2x16 block of a 8x8x16 slice. The times are simulated.
128 devices in a mesh: grp: 4 (over x, y), gx: 32 (over z, core).
Axes of the slice: x: 2, y: 2, z: 16, core: 2. Of those that a mesh axis runs over, the one named last changes fastest.
The devices are a block of a 8x8x16 slice.
Arguments:
- wave_now: float32 [12, 512, 64, 256], P('grp', 'gx'), parts along dimension 0
- wave_prev: float32 [12, 512, 64, 256], P('grp', 'gx'), parts along dimension 0
- velocity: float32 [2048, 64, 256], P(('grp', 'gx')), parts along dimension 0, may hold values from 0.05 to 0.18
- snapshots: float32 [12, 2, 512, 64, 256], P('grp', None, 'gx'), parts along dimension 0, may hold values from -6 to 6
- traces: float32 [16, 1024], P('grp'), parts along dimension 0, may hold values from -18 to 18
- recv_x: int32 [4096], P('grp'), parts along dimension 0, may hold values from 0 to 511
- recv_y: int32 [4096], P('grp'), parts along dimension 0, may hold values from 0 to 63
- recv_z: int32 [4096], P('grp'), parts along dimension 0, may hold values from 0 to 255
- recv_shot: int32 [4096], P('grp'), parts along dimension 0, may hold values from 0 to 2
- snap_step: int32 [16, 3], P('grp'), parts along dimension 0, may hold values from 0 to 1
Outputs:
- image: float32 [2048, 64, 256], P(('grp', 'gx')), parts along dimension 0
- final_now: float32 [12, 512, 64, 256], P('grp', 'gx'), parts along dimension 0
- final_prev: float32 [12, 512, 64, 256], P('grp', 'gx'), parts along dimension 0
- energies: float32 [16, 3], P('grp'), parts along dimension 0
There are 4 independent parts, one for each index of `grp`. A program takes and returns all parts, laid end to end along the dimension named above; each array names one. Nothing has to cross between parts.
All inputs are finite; a program needn't handle non-finite values.
Results may differ from a plain program's by a relative error of at most 0.00021.
Values sent between devices are 32-bit elements; how exact they have to be, the bound alone decides.
A program may use at most 128 MiB of HBM per device.

v0:
```python
import jax
import jax.numpy as jnp
from jax import lax
from jax.sharding import PartitionSpec as P

COEFS = (-205.0 / 72.0, 8.0 / 5.0, -1.0 / 5.0, 8.0 / 315.0, -1.0 / 560.0)


def padded_2(block, sides, width):
    for axis, dim in sides:
        count = lax.axis_size(axis)
        forward = [(i, i + 1) for i in range(count - 1)]
        backward = [(target, source) for source, target in forward]
        low = lax.ppermute(
            lax.slice_in_dim(block, block.shape[dim] - width, None, axis=dim), axis, forward
        )
        high = lax.ppermute(lax.slice_in_dim(block, 0, width, axis=dim), axis, backward)
        block = jnp.concatenate([low, block, high], axis=dim)
    return block


def from_everyone(array, axis):
    size = lax.axis_size(axis)
    return lax.all_to_all(
        jnp.broadcast_to(array[None], (size, *array.shape)), axis, 0, 0, tiled=True
    )


def taken_together(array, axis):
    everything = from_everyone(array, axis)
    return jnp.sum(everything, axis=0)


def laplace(widened):
    length = widened.shape[1] - 8
    depth_y, depth_z = (widened.shape[2], widened.shape[3])
    padded = jnp.pad(widened, ((0, 0), (0, 0), (4, 4), (4, 4)))

    def cut(shift_x, shift_y, shift_z):
        return padded[
            :,
            4 + shift_x : 4 + shift_x + length,
            4 + shift_y : 4 + shift_y + depth_y,
            4 + shift_z : 4 + shift_z + depth_z,
        ]

    total = 3.0 * COEFS[0] * cut(0, 0, 0)
    for reach in range(1, 5):
        total = total + COEFS[reach] * (
            cut(reach, 0, 0)
            + cut(-reach, 0, 0)
            + cut(0, reach, 0)
            + cut(0, -reach, 0)
            + cut(0, 0, reach)
            + cut(0, 0, -reach)
        )
    return total


def inject(field, region, lower, samples, recv_x, recv_y, recv_z, recv_shot):
    length = field.shape[1]
    local = recv_x - lower
    inside = (local >= 0) & (local < length)
    place = jnp.where(inside, local, length)
    speeds = region[jnp.clip(place, 0, length - 1), recv_y, recv_z]
    source = jnp.where(inside, samples * speeds, 0.0)
    return field.at[recv_shot, place, recv_y, recv_z].add(source, mode="drop")


def per_device(
    wave_now, wave_prev, velocity, snapshots, traces, recv_x, recv_y, recv_z, recv_shot, snap_step
):
    slab_cells = velocity.shape[0]
    start = lax.axis_index("gx") * slab_cells
    cells = slab_cells * lax.axis_size("gx") * velocity.shape[1] * velocity.shape[2]
    shot_ids = jnp.arange(wave_now.shape[0], dtype=jnp.int32)
    steps = traces.shape[0]
    image = jnp.zeros(velocity.shape, jnp.float32)
    partial_value = []
    corrs = []

    def record(step, fresh):
        local = jnp.sum(fresh * fresh, axis=(1, 2, 3))
        chosen = snapshots[shot_ids, snap_step[step]]
        corr = chosen * fresh
        partial_value.append(local)
        corrs.append(corr)

    current, previous = (wave_now, wave_prev)
    speeds_wide = padded_2(velocity, (("gx", 0),), 4)
    prev_wide = padded_2(previous, (("gx", 1),), 4)
    for couple in range(steps // 2):
        now_wide = padded_2(current, (("gx", 1),), 8)
        first = 2.0 * now_wide[:, 4:-4] - prev_wide + speeds_wide[None] * laplace(now_wide)
        first = inject(
            first, speeds_wide, start - 4, traces[2 * couple], recv_x, recv_y, recv_z, recv_shot
        )
        record(2 * couple, first[:, 4:-4])
        second = 2.0 * first[:, 4:-4] - current + velocity[None] * laplace(first)
        second = inject(
            second, velocity, start, traces[2 * couple + 1], recv_x, recv_y, recv_z, recv_shot
        )
        record(2 * couple + 1, second)
        prev_wide = first
        previous, current = (first[:, 4:-4], second)
    energies = taken_together(jnp.stack(partial_value), "gx")
    weights = 1.0 / jnp.sqrt(energies / cells + 1e-06)
    result = image
    for step in range(steps):
        result = result + jnp.sum(weights[step][:, None, None, None] * corrs[step], axis=0)
    return (result, current, previous, energies)


def solution(mesh):
    placed = (
        P("grp", "gx", None, None),
        P("grp", "gx", None, None),
        P(("grp", "gx"), None, None),
        P("grp", None, "gx", None, None),
        P("grp", None),
        P("grp"),
        P("grp"),
        P("grp"),
        P("grp"),
        P("grp", None),
    )
    return jax.shard_map(
        per_device,
        mesh=mesh,
        in_specs=placed,
        out_specs=(
            P(("grp", "gx"), None, None),
            P("grp", "gx", None, None),
            P("grp", "gx", None, None),
            P("grp", None),
        ),
        check_vma=False,
    )
```

profile of v0, /device:TPU:69, one launch (start us, length us, event | category | flops | bytes accessed | tf_op | source)
XLA Modules:
  0.0 355.8 jit_solution(14570385578497149912)
XLA Ops:
  1.7 5.1 %collective-permute-start.4 = (f32[4,64,256]{2,1,0:T(8,128)S(1)}, f32[4,64,256]{2,1,0:T(8,128)S(1)}, u32[]{:S(2)}, u32[]{:S(2)}) collective-permute-start(f32[4,64,256]{2,1,0:T(8,128)S(1)} %get-tuple-element.37), channel_id=1, source_target_pairs={{0,1},{1,2},{2,3},{3,4},{4,5},{5,6},{6,7},{7,8},{8,9},{9,10},{10,1... | collective-permute-start | bytes 786440 | tf_op jit(solution)/shard_map/ppermute | solution.py:14
  6.8 8.3 %collective-permute-start.5 = (f32[4,64,256]{2,1,0:T(8,128)S(1)}, f32[4,64,256]{2,1,0:T(8,128)S(1)}, u32[]{:S(2)}, u32[]{:S(2)}) collective-permute-start(f32[4,64,256]{2,1,0:T(8,128)S(1)} %get-tuple-element.36), channel_id=1, source_target_pairs={{1,0},{2,1},{3,2},{4,3},{5,4},{6,5},{7,6},{8,7},{9,8},{10,9},{11,1... | collective-permute-start | bytes 786440 | tf_op jit(solution)/shard_map/ppermute | solution.py:17
  15.2 3.9 %fusion.126 = (f32[3,8,64,256]{3,2,1,0:T(8,128)}, f32[3,8,64,256]{3,2,1,0:T(8,128)}) fusion(f32[3,16,64,256]{3,2,1,0:T(8,128)} %param.10), kind=kLoop, calls=%fused_computation.275 | loop fusion | bytes 6291456 | tf_op jit(solution)/shard_map/slice | solution.py:17
  21.2 3.6 %collective-permute-start.1 = (f32[3,8,64,256]{3,2,1,0:T(8,128)}, f32[3,8,64,256]{3,2,1,0:T(8,128)}, u32[]{:S(2)}, u32[]{:S(2)}) collective-permute-start(f32[3,8,64,256]{3,2,1,0:T(8,128)} %get-tuple-element.34), channel_id=1, source_target_pairs={{1,0},{2,1},{3,2},{4,3},{5,4},{6,5},{7,6},{8,7},{9,8},{10,9},{11,1... | collective-permute-start | bytes 4718600 | tf_op jit(solution)/shard_map/ppermute | solution.py:17
  28.6 10.5 %gather_fusion.1 = f32[1024]{0:T(1024)S(1)} fusion(f32[16,64,256]{2,1,0:T(8,128)S(1)} %copy-done, s32[1024]{0:T(1024)S(1)} %bitcast.52), kind=kCustom, calls=%fused_computation.1 | custom fusion | bytes 20480 | tf_op jit(solution)/shard_map/gather | solution.py:65
  39.2 3.3 collective-permute-start.3
  42.6 10.5 %gather_fusion = f32[1024]{0:T(1024)S(1)} fusion(f32[24,64,256]{2,1,0:T(8,128)S(1)} %constant_dynamic-update-slice_fusion.3, s32[1024]{0:T(1024)S(1)} %bitcast.51), kind=kCustom, calls=%fused_computation | custom fusion | bytes 20480 | tf_op jit(solution)/shard_map/gather | solution.py:65
  57.4 16.5 %fusion.10 = f32[3,24,64,256]{3,2,1,0:T(8,128)} fusion(f32[3,32,64,256]{3,2,1,0:T(8,128)S(1)} %constant_dynamic-update-slice_fusion, f32[3,4,64,256]{3,2,1,0:T(8,128)} %collective-permute-done.3, f32[3,16,64,256]{3,2,1,0:T(8,128)} %param.11, f32[3,4,64,256]{3,2,1,0:T(8,128)} %collective-permute-done.2, f32[3,8,64,256]{3,2,1,0:T(8,128)} %collective-permute-done.1, ...), kind=kLoop, calls=%fused_computation.84 | loop fusion | flops 43646976 | bytes 56623104 | tf_op jit(solution)/shard_map/add | solution.py:94
  73.9 7.0 %copy.22 = f32[576,2,8,128]{3,1,2,0:T(2,128)} copy(f32[576,2,8,128]{3,2,1,0:T(8,128)} %bitcast.56) | data formatting | bytes 9437184
  80.8 10.0 %scatter_fusion = f32[1179648]{0:T(1024)} fusion(f32[1179648]{0:T(1024)} %bitcast.54, s32[1024]{0:T(1024)S(1)} %get-tuple-element.59, f32[1024]{0:T(1024)S(1)} %get-tuple-element.48), kind=kCustom, calls=%fused_computation.6 | custom fusion | flops 1024 | bytes 16384
  90.8 6.4 %reshape.130 = f32[3,24,64,256]{3,2,1,0:T(8,128)} reshape(f32[1179648]{0:T(1024)} %scatter_fusion) | data formatting | bytes 9437184 | tf_op jit(solution)/shard_map/scatter-add | solution.py:67
  97.2 35.7 %multiply_reduce_fusion.7 = (f32[3]{0:T(128)S(1)}, f32[3,16,64,256]{3,2,1,0:T(8,128)}) fusion(f32[3,24,64,256]{3,2,1,0:T(8,128)} %reshape.130, f32[16,64,256]{2,1,0:T(8,128)S(1)} %copy-done.1, f32[3,16,64,256]{3,2,1,0:T(8,128)} %param.10), kind=kLoop, calls=%fused_computation.202 | loop fusion | flops 27525116 | bytes 40370188 | tf_op jit(solution)/shard_map/reduce_sum | solution.py:83
  132.9 5.2 %copy.23 = f32[384,2,8,128]{3,1,2,0:T(2,128)} copy(f32[384,2,8,128]{3,2,1,0:T(8,128)} %bitcast.59) | data formatting | bytes 6291456
  138.1 9.0 %scatter_fusion.1 = f32[786432]{0:T(1024)} fusion(f32[786432]{0:T(1024)} %bitcast.28, s32[1024]{0:T(1024)S(1)} %get-tuple-element.58, f32[1024]{0:T(1024)S(1)} %get-tuple-element.43), kind=kCustom, calls=%fused_computation.7 | custom fusion | flops 1024 | bytes 16384
  147.0 3.1 reshape.134
  155.2 15.0 %collective-permute-done.6 = f32[3,8,64,256]{3,2,1,0:T(8,128)S(1)} collective-permute-done((f32[3,8,64,256]{3,2,1,0:T(8,128)S(1)}, f32[3,8,64,256]{3,2,1,0:T(8,128)S(1)}, u32[]{:S(2)}, u32[]{:S(2)}) %collective-permute-start.6) | collective-permute-done | bytes 1572896 | tf_op jit(solution)/shard_map/ppermute | solution.py:14
  177.1 42.4 %fusion.36 = f32[3,24,64,256]{3,2,1,0:T(8,128)} fusion(f32[3,32,64,256]{3,2,1,0:T(8,128)} %constant_dynamic-update-slice_fusion.6, f32[3,8,64,256]{3,2,1,0:T(8,128)} %copy-done.12, f32[3,16,64,256]{3,2,1,0:T(8,128)S(1)} %reshape.134, f32[3,8,64,256]{3,2,1,0:T(8,128)} %copy-done.11, f32[3,24,64,256]{3,2,1,0:T(8,128)S(1)} %bitcast.50, ...), kind=kLoop, calls=%fused_computation.110 | loop fusion | flops 41287680 | bytes 56623104 | tf_op jit(solution)/shard_map/add | solution.py:94
  219.5 6.9 %copy.24 = f32[576,2,8,128]{3,1,2,0:T(2,128)} copy(f32[576,2,8,128]{3,2,1,0:T(8,128)} %bitcast.57) | data formatting | bytes 9437184
  226.4 9.9 %scatter_fusion.2 = f32[1179648]{0:T(1024)} fusion(f32[1179648]{0:T(1024)} %bitcast.53, s32[1024]{0:T(1024)S(1)} %get-tuple-element.59, f32[1024]{0:T(1024)S(1)} %get-tuple-element.49), kind=kCustom, calls=%fused_computation.8 | custom fusion | flops 1024 | bytes 16384
  236.3 6.3 %reshape.138 = f32[3,24,64,256]{3,2,1,0:T(8,128)} reshape(f32[1179648]{0:T(1024)} %scatter_fusion.2) | data formatting | bytes 9437184 | tf_op jit(solution)/shard_map/scatter-add | solution.py:67
  242.5 4.0 %multiply_reduce_fusion.5 = (f32[3]{0:T(128)S(1)}, f32[3,16,64,256]{3,2,1,0:T(8,128)}) fusion(f32[3,24,64,256]{3,2,1,0:T(8,128)} %reshape.138), kind=kLoop, calls=%fused_computation.200 | loop fusion | flops 1572861 | bytes 6291468 | tf_op jit(solution)/shard_map/reduce_sum | solution.py:83
  246.5 35.2 %multiply_reduce_fusion.6 = (f32[3]{0:T(128)S(1)}, f32[3,16,64,256]{3,2,1,0:T(8,128)}) fusion(f32[3,16,64,256]{3,2,1,0:T(8,128)S(1)} %reshape.134, f32[3,24,64,256]{3,2,1,0:T(8,128)} %reshape.138, f32[3,16,64,256]{3,2,1,0:T(8,128)} %get-tuple-element.25, f32[16,64,256]{2,1,0:T(8,128)} %param.12), kind=kLoop, calls=%fused_computation.201 | loop fusion | flops 27525116 | bytes 40370188 | tf_op jit(solution)/shard_map/reduce_sum | solution.py:83
  281.7 5.2 %copy.25 = f32[384,2,8,128]{3,1,2,0:T(2,128)} copy(f32[384,2,8,128]{3,2,1,0:T(8,128)} %bitcast.58) | data formatting | bytes 6291456
  286.9 9.0 %scatter_fusion.3 = f32[786432]{0:T(1024)} fusion(f32[786432]{0:T(1024)} %bitcast.55, s32[1024]{0:T(1024)S(1)} %get-tuple-element.58, f32[1024]{0:T(1024)S(1)} %get-tuple-element.42), kind=kCustom, calls=%fused_computation.9 | custom fusion | flops 1024 | bytes 16384
  295.9 4.8 %reshape.142 = f32[3,16,64,256]{3,2,1,0:T(8,128)} reshape(f32[786432]{0:T(1024)} %scatter_fusion.3) | data formatting | bytes 6291456 | tf_op jit(solution)/shard_map/scatter-add | solution.py:67
  303.7 18.2 %all-to-all-start = ((f32[32,4,3]{1,2,0:T(4,128)}), f32[32,4,3]{1,2,0:T(4,128)S(1)}, u32[]{:S(2)}, u32[]{:S(2)}) async-start(f32[32,4,3]{1,2,0:T(4,128)} %broadcast_in_dim.36), calls=%async_computation | async-start | bytes 131072 | tf_op jit(solution)/shard_map/all_to_all | solution.py:24
  322.0 5.2 %gather_fusion.3 = f32[3,16,64,256]{3,2,1,0:T(8,128)} fusion(f32[3,2,16,64,256]{4,3,2,1,0:T(8,128)} %param.13, s32[3]{0:T(128)S(1)} %get-tuple-element.54), kind=kCustom, calls=%fused_computation.3 | custom fusion | bytes 6291480 | tf_op jit(solution)/shard_map/gather | solution.py:84
  327.2 5.4 %gather_fusion.2 = f32[3,16,64,256]{3,2,1,0:T(8,128)} fusion(f32[3,2,16,64,256]{4,3,2,1,0:T(8,128)} %param.13, s32[3]{0:T(128)S(1)} %get-tuple-element.55), kind=kCustom, calls=%fused_computation.2 | custom fusion | bytes 6291480 | tf_op jit(solution)/shard_map/gather | solution.py:84
  332.6 5.3 %gather_fusion.4 = f32[3,16,64,256]{3,2,1,0:T(8,128)} fusion(f32[3,2,16,64,256]{4,3,2,1,0:T(8,128)} %param.13, s32[3]{0:T(128)S(1)} %get-tuple-element.57), kind=kCustom, calls=%fused_computation.4 | custom fusion | bytes 6291480 | tf_op jit(solution)/shard_map/gather | solution.py:84
  337.9 5.3 %gather_fusion.5 = f32[3,16,64,256]{3,2,1,0:T(8,128)} fusion(f32[3,2,16,64,256]{4,3,2,1,0:T(8,128)} %param.13, s32[3]{0:T(128)S(1)} %get-tuple-element.56), kind=kCustom, calls=%fused_computation.5 | custom fusion | bytes 6291480 | tf_op jit(solution)/shard_map/gather | solution.py:84
  344.1 2.9 multiply_reduce_fusion.2
  347.0 2.9 multiply_reduce_fusion.3
  (97 shorter events, 32.8 us)
Async XLA Ops:
  1.7 37.5 %collective-permute-start.4 = (f32[4,64,256]{2,1,0:T(8,128)S(1)}, f32[4,64,256]{2,1,0:T(8,128)S(1)}, u32[]{:S(2)}, u32[]{:S(2)}) collective-permute-start(f32[4,64,256]{2,1,0:T(8,128)S(1)} %get-tuple-element.37), channel_id=1, source_target_pairs={{0,1},{1,2},{2,3},{3,4},{4,5},{5,6},{6,7},{7,8},{8,9},{9,10},{10,1... | collective-permute-start | bytes 786440 | tf_op jit(solution)/shard_map/ppermute | solution.py:14
  6.8 18.0 %copy-start.10 = (f32[3,16,64,256]{3,2,1,0:T(8,128)S(1)}, f32[3,16,64,256]{3,2,1,0:T(8,128)}, u32[]{:S(2)}) copy-start(f32[3,16,64,256]{3,2,1,0:T(8,128)} %param.11) | copy-start | bytes 9437188
  6.8 35.8 %collective-permute-start.5 = (f32[4,64,256]{2,1,0:T(8,128)S(1)}, f32[4,64,256]{2,1,0:T(8,128)S(1)}, u32[]{:S(2)}, u32[]{:S(2)}) collective-permute-start(f32[4,64,256]{2,1,0:T(8,128)S(1)} %get-tuple-element.36), channel_id=1, source_target_pairs={{1,0},{2,1},{3,2},{4,3},{5,4},{6,5},{7,6},{8,7},{9,8},{10,9},{11,1... | collective-permute-start | bytes 786440 | tf_op jit(solution)/shard_map/ppermute | solution.py:17
  19.1 9.1 %copy-start.15 = (s32[1024]{0:T(1024)S(1)}, s32[1024]{0:T(1024)}, u32[]{:S(2)}) copy-start(s32[1024]{0:T(1024)} %param.16) | copy-start | bytes 12292
  19.1 9.1 %copy-start.16 = (s32[1024]{0:T(1024)S(1)}, s32[1024]{0:T(1024)}, u32[]{:S(2)}) copy-start(s32[1024]{0:T(1024)} %param.17) | copy-start | bytes 12292
  19.1 9.2 %copy-start.14 = (s32[1024]{0:T(1024)S(1)}, s32[1024]{0:T(1024)}, u32[]{:S(2)}) copy-start(s32[1024]{0:T(1024)} %param.15) | copy-start | bytes 12292
  19.1 9.2 %copy-start.17 = (s32[1024]{0:T(1024)S(1)}, s32[1024]{0:T(1024)}, u32[]{:S(2)}) copy-start(s32[1024]{0:T(1024)} %param.18) | copy-start | bytes 12292
  19.1 9.2 %copy-start.19 = (s32[4]{0:T(128)S(1)}, s32[4]{0:T(128)}, u32[]{:S(2)}) copy-start(s32[4]{0:T(128)} %constant.73) | copy-start | bytes 52
  19.1 9.2 %copy-start.20 = (s32[4]{0:T(128)S(1)}, s32[4]{0:T(128)}, u32[]{:S(2)}) copy-start(s32[4]{0:T(128)} %constant.79) | copy-start | bytes 52
  19.1 9.3 %copy-start.13 = (f32[4,1024]{1,0:T(4,128)S(1)}, f32[4,1024]{1,0:T(4,128)}, u32[]{:S(2)}) copy-start(f32[4,1024]{1,0:T(4,128)} %param.14) | copy-start | bytes 49156
  19.1 9.4 %copy-start.21 = (s32[4]{0:T(128)S(1)}, s32[4]{0:T(128)}, u32[]{:S(2)}) copy-start(s32[4]{0:T(128)} %constant.70) | copy-start | bytes 52
  19.1 9.4 %copy-start.22 = (s32[4]{0:T(128)S(1)}, s32[4]{0:T(128)}, u32[]{:S(2)}) copy-start(s32[4]{0:T(128)} %constant.76) | copy-start | bytes 52
  19.1 9.5 %copy-start = (f32[16,64,256]{2,1,0:T(8,128)S(1)}, f32[16,64,256]{2,1,0:T(8,128)}, u32[]{:S(2)}) copy-start(f32[16,64,256]{2,1,0:T(8,128)} %param.12) | copy-start | bytes 3145732
  19.1 34.1 %collective-permute-start = (f32[3,8,64,256]{3,2,1,0:T(8,128)}, f32[3,8,64,256]{3,2,1,0:T(8,128)}, u32[]{:S(2)}, u32[]{:S(2)}) collective-permute-start(f32[3,8,64,256]{3,2,1,0:T(8,128)} %get-tuple-element.35), channel_id=1, source_target_pairs={{0,1},{1,2},{2,3},{3,4},{4,5},{5,6},{6,7},{7,8},{8,9},{9,10},{10,1... | collective-permute-start | bytes 4718600 | tf_op jit(solution)/shard_map/ppermute | solution.py:14
  21.2 34.6 %collective-permute-start.1 = (f32[3,8,64,256]{3,2,1,0:T(8,128)}, f32[3,8,64,256]{3,2,1,0:T(8,128)}, u32[]{:S(2)}, u32[]{:S(2)}) collective-permute-start(f32[3,8,64,256]{3,2,1,0:T(8,128)} %get-tuple-element.34), channel_id=1, source_target_pairs={{1,0},{2,1},{3,2},{4,3},{5,4},{6,5},{7,6},{8,7},{9,8},{10,9},{11,1... | collective-permute-start | bytes 4718600 | tf_op jit(solution)/shard_map/ppermute | solution.py:17
  26.1 31.2 %collective-permute-start.2 = (f32[3,4,64,256]{3,2,1,0:T(8,128)}, f32[3,4,64,256]{3,2,1,0:T(8,128)}, u32[]{:S(2)}, u32[]{:S(2)}) collective-permute-start(f32[3,4,64,256]{3,2,1,0:T(8,128)} %get-tuple-element.32), channel_id=1, source_target_pairs={{0,1},{1,2},{2,3},{3,4},{4,5},{5,6},{6,7},{7,8},{8,9},{9,10},{10,1... | collective-permute-start | bytes 2359304 | tf_op jit(solution)/shard_map/ppermute | solution.py:14
  39.2 18.2 %collective-permute-start.3 = (f32[3,4,64,256]{3,2,1,0:T(8,128)}, f32[3,4,64,256]{3,2,1,0:T(8,128)}, u32[]{:S(2)}, u32[]{:S(2)}) collective-permute-start(f32[3,4,64,256]{3,2,1,0:T(8,128)} %get-tuple-element.33), channel_id=1, source_target_pairs={{1,0},{2,1},{3,2},{4,3},{5,4},{6,5},{7,6},{8,7},{9,8},{10,9},{11,1... | collective-permute-start | bytes 2359304 | tf_op jit(solution)/shard_map/ppermute | solution.py:17
  42.6 10.6 %copy-start.3 = (f32[24,64,256]{2,1,0:T(8,128)}, f32[24,64,256]{2,1,0:T(8,128)S(1)}, u32[]{:S(2)}) copy-start(f32[24,64,256]{2,1,0:T(8,128)S(1)} %constant_dynamic-update-slice_fusion.3) | copy-start | bytes 4718596
  53.2 2.4 copy-start.2
  90.8 6.4 %copy-start.1 = (f32[16,64,256]{2,1,0:T(8,128)S(1)}, f32[16,64,256]{2,1,0:T(8,128)}, u32[]{:S(2)}) copy-start(f32[16,64,256]{2,1,0:T(8,128)} %param.12) | copy-start | bytes 3145732
  150.5 19.7 %collective-permute-start.6 = (f32[3,8,64,256]{3,2,1,0:T(8,128)S(1)}, f32[3,8,64,256]{3,2,1,0:T(8,128)S(1)}, u32[]{:S(2)}, u32[]{:S(2)}) collective-permute-start(f32[3,8,64,256]{3,2,1,0:T(8,128)S(1)} %get-tuple-element.31), channel_id=1, source_target_pairs={{0,1},{1,2},{2,3},{3,4},{4,5},{5,6},{6,7},{7,8},{8,9},{9,10},{10,1... | collective-permute-start | bytes 4718600 | tf_op jit(solution)/shard_map/ppermute | solution.py:14
  152.8 21.8 %collective-permute-start.7 = (f32[3,8,64,256]{3,2,1,0:T(8,128)S(1)}, f32[3,8,64,256]{3,2,1,0:T(8,128)S(1)}, u32[]{:S(2)}, u32[]{:S(2)}) collective-permute-start(f32[3,8,64,256]{3,2,1,0:T(8,128)S(1)} %get-tuple-element.30), channel_id=1, source_target_pairs={{1,0},{2,1},{3,2},{4,3},{5,4},{6,5},{7,6},{8,7},{9,8},{10,9},{11,1... | collective-permute-start | bytes 4718600 | tf_op jit(solution)/shard_map/ppermute | solution.py:17
  171.3 5.7 %slice-start = ((s8[4718592]{0:T(1024)(128)(4,1)}), s8[4194304]{0:T(1024)(128)(4,1)S(1)}, s32[]{:S(2)}) async-start(s8[4718592]{0:T(1024)(128)(4,1)} %bitcast.49), calls=%async_computation.1 | async-start | bytes 8388608
  172.6 4.5 %slice-start.1 = ((s8[4718592]{0:T(1024)(128)(4,1)}), s8[524288]{0:T(1024)(128)(4,1)S(1)}, s32[]{:S(2)}) async-start(s8[4718592]{0:T(1024)(128)(4,1)} %bitcast.49), calls=%async_computation.2 | async-start | bytes 1048576
  174.5 2.6 copy-start.4
  300.7 21.3 %copy-start.18 = (s32[4,3]{1,0:T(4,128)S(1)}, s32[4,3]{1,0:T(4,128)}, u32[]{:S(2)}) copy-start(s32[4,3]{1,0:T(4,128)} %param.19) | copy-start | bytes 148
  303.7 39.4 %all-to-all-start = ((f32[32,4,3]{1,2,0:T(4,128)}), f32[32,4,3]{1,2,0:T(4,128)S(1)}, u32[]{:S(2)}, u32[]{:S(2)}) async-start(f32[32,4,3]{1,2,0:T(4,128)} %broadcast_in_dim.36), calls=%async_computation | async-start | bytes 131072 | tf_op jit(solution)/shard_map/all_to_all | solution.py:24
  344.1 2.9 copy-start.9
  347.0 2.9 copy-start.6
  347.0 3.8 %copy-start.8 = (f32[3,16,64,256]{3,2,1,0:T(8,128)S(1)}, f32[3,16,64,256]{3,2,1,0:T(8,128)}, u32[]{:S(2)}) copy-start(f32[3,16,64,256]{3,2,1,0:T(8,128)} %gather_fusion.4) | copy-start | bytes 9437188
  350.8 1.9 copy-start.5
  350.8 2.8 copy-start.7
  (2 other events, 2.3 us)
where the time goes:
time: 357 us; the launch traced here: 356 us
  other arithmetic  183 us (51%)
  local copies, waits for them, and re-layouts  109 us (31%)
  starting transfers between devices  47.3 us (13%)
  waiting for transfers between devices  15.1 us (4%)
    reduce_sum x4, other arithmetic, record(): local = jnp.sum(fresh * fresh, axis=(1, 2, 3))  77.2 us
    add x2, other arithmetic, per_device(): 2.0 * now_wide[:, 4:-4] - prev_wide + speeds_wide[None] * laplace(now_wide)  58.9 us
    unnamed x8, other arithmetic  38 us
    unnamed x61, local copies, waits for them, and re-layouts  35.9 us
    gather x4, local copies, waits for them, and re-layouts, record(): chosen = snapshots[shot_ids, snap_step[step]]  21.2 us
    gather x2, local copies, waits for them, and re-layouts, inject(): speeds = region[jnp.clip(place, 0, length - 1), recv_y, recv_z]  21.1 us
    scatter-add x4, local copies, waits for them, and re-layouts, inject(): return field.at[recv_shot, place, recv_y, recv_z].add(source, mode='drop')  20.6 us
    all_to_all x1, starting transfers between devices, from_everyone(): lax.all_to_all(jnp.broadcast_to(array[None], (size, *array.shape)), axis,...  18.2 us
  transfers between devices with their start and end apart: 9, of which 2 were waited for; matrix products, arithmetic and copies ran while one was open for 15% of the time, Pallas kernels for 0%

commit v1 on v0

v1 whole, which is shorter than its diff:
```python
import functools

import jax
import jax.numpy as jnp
from jax import lax
from jax.experimental import pallas as pl
from jax.experimental.pallas import tpu as pltpu
from jax.sharding import PartitionSpec as P

MESH = pl.DeviceIdType.MESH
SCALE = 5040.0
CENTRE = -43050.0
REACH = (0.0, 8064.0, -1008.0, 128.0, -9.0)
HALO = 4
ROWS = 4
F32 = jnp.float32
BF16 = jnp.bfloat16


def band(size, period):
    row = lax.broadcasted_iota(jnp.int32, (size, size), 0)
    col = lax.broadcasted_iota(jnp.int32, (size, size), 1)
    gap = jnp.abs(row - col)
    same = (row // period) == (col // period)
    value = jnp.zeros((size, size), F32)
    for k in range(1, HALO + 1):
        value = jnp.where((gap == k) & same, REACH[k], value)
    return value.astype(BF16)


def dot(a, b, dims=((1,), (0,))):
    return lax.dot_general(a, b, (dims, ((), ())), preferred_element_type=F32)


def kernel(
    n,
    now_hbm,
    prev_hbm,
    vel_hbm,
    snap_hbm,
    traces,
    recv_x,
    recv_y,
    recv_z,
    recv_shot,
    snap_step,
    image_hbm,
    last_hbm,
    before_hbm,
    energy_out,
    w,
    vel,
    snap,
    corr,
    onehot,
    amps,
    band_y,
    band_z,
    squares,
    image,
    row_mine,
    row_partner,
    row_chip,
    rows_all,
    load_edge,
    load_mid,
    load_prev,
    load_vel,
    load_snap,
    send_sem,
    recv_sem,
    ready_sem,
    pair_send,
    pair_recv,
    all_send,
    all_recv,
    out_last,
    out_before,
    out_image,
):
    shots, slab, ny, nz = now_hbm.shape
    steps, count = traces.shape
    blocks = slab // ROWS
    low, high = HALO, HALO + slab
    me = lax.axis_index("gx")
    right, left = lax.rem(me + 1, n), lax.rem(me + n - 1, n)

    barrier = pltpu.get_barrier_semaphore()
    for other in (left, right):
        pl.semaphore_signal(barrier, inc=1, device_id={"gx": other}, device_id_type=MESH)

    def edge_load(s, side):
        at = 0 if side == 0 else slab - HALO
        return pltpu.make_async_copy(
            now_hbm.at[s, pl.ds(at, HALO)], w.at[0, s, pl.ds(low + at, HALO)], load_edge.at[side, s]
        )

    def mid_load(s):
        return pltpu.make_async_copy(
            now_hbm.at[s, pl.ds(HALO, slab - 2 * HALO)],
            w.at[0, s, pl.ds(low + HALO, slab - 2 * HALO)],
            load_mid.at[s],
        )

    def prev_load(s):
        return pltpu.make_async_copy(prev_hbm.at[s], w.at[1, s, pl.ds(low, slab)], load_prev.at[s])

    def snap_load(s):
        return pltpu.make_async_copy(snap_hbm.at[s], snap.at[s], load_snap.at[s])

    vel_load = pltpu.make_async_copy(vel_hbm, vel, load_vel)

    for s in range(shots):
        for side in range(2):
            edge_load(s, side).start()
    vel_load.start()
    for s in range(shots):
        mid_load(s).start()
        prev_load(s).start()
    for s in range(shots):
        snap_load(s).start()

    def halo_copy(t, s, side):
        parity = lax.rem(t, 2)
        if side == 0:
            source, target, device = low, high, left
        else:
            source, target, device = high - HALO, 0, right
        return pltpu.make_async_remote_copy(
            src_ref=w.at[parity, s, pl.ds(source, HALO)],
            dst_ref=w.at[parity, s, pl.ds(target, HALO)],
            send_sem=send_sem.at[side, t, s],
            recv_sem=recv_sem.at[side, t, s],
            device_id={"gx": device},
            device_id_type=MESH,
        )

    has = (me > 0, me < n - 1)

    pl.semaphore_wait(barrier, 2)
    for s in range(shots):
        for side in range(2):
            edge_load(s, side).wait()

            @pl.when(has[side])
            def _():
                halo_copy(0, s, side).start()

    zeros = jnp.zeros((HALO, ny, nz), F32)
    for side, at in ((0, 0), (1, high)):

        @pl.when(jnp.logical_not(has[side]))
        def _():
            for parity in range(2):
                for s in range(shots):
                    w[parity, s, pl.ds(at, HALO)] = zeros

    band_y[...] = band(ROWS * ny, ny)
    band_z[...] = band(nz, nz)
    local = recv_x[...] - me * slab
    inside = (local >= 0) & (local < slab)
    place = jnp.where(inside, (recv_shot[...] * slab + local) * ny + recv_y[...], -1)

    def fill_onehot(b, carry):
        index = lax.broadcasted_iota(jnp.int32, (ROWS * ny, count), 0) + b * (ROWS * ny)
        onehot[b] = jnp.where(index == place, 1.0, 0.0).astype(BF16)
        return carry

    lax.fori_loop(0, shots * blocks, fill_onehot, 0)
    along = lax.broadcasted_iota(jnp.int32, (nz, count), 0) == recv_z[...]
    for t in range(steps):
        amp = traces[t : t + 1, :] * SCALE
        top = amp.astype(BF16).astype(F32)
        amps[t, 0] = jnp.where(along, top, 0.0).astype(BF16)
        amps[t, 1] = jnp.where(along, amp - top, 0.0).astype(BF16)

    vel_load.wait()
    vel[...] = vel[...] * (1.0 / SCALE)

    def fold(value):
        return jnp.sum(value.reshape(ny // 8, 8, nz), axis=0)

    def record(t, s, x, fresh):
        chosen = snap[s, snap_step[t, s], x]
        corr[t, s, x] = chosen * fresh
        return fold(fresh * fresh)

    def block_stage(t, s):
        cur = lax.rem(t, 2)
        nxt = 1 - cur
        for b in range(blocks):
            inner = 0 < b < blocks - 1
            x0 = b * ROWS
            v = w[cur, s, pl.ds(low + x0, ROWS)].reshape(ROWS * ny, nz)
            top = v.astype(BF16)
            rest = (v - top.astype(F32)).astype(BF16)
            acc = dot(top, band_z[...]) + dot(rest, band_z[...])
            acc = acc + dot(band_y[...], top) + dot(band_y[...], rest)
            hot = onehot[s * blocks + b]
            acc = acc + dot(hot, amps[t, 0], ((1,), (1,))) + dot(hot, amps[t, 1], ((1,), (1,)))
            acc = acc.reshape(ROWS, ny, nz)
            total = jnp.zeros((8, nz), F32)
            for i in range(ROWS):
                x = x0 + i
                centre = w[cur, s, low + x]
                value = acc[i] + CENTRE * centre
                for k in range(1, HALO + 1):
                    near = []
                    if x + k < slab:
                        near.append(w[cur, s, low + x + k])
                    if x - k >= 0:
                        near.append(w[cur, s, low + x - k])
                    pair = near[0] + near[1] if len(near) == 2 else near[0]
                    value = value + REACH[k] * pair
                fresh = 2.0 * centre - w[nxt, s, low + x] + vel[x] * value
                w[nxt, s, low + x] = fresh
                if inner:
                    total = total + record(t, s, x, fresh)
            if inner:
                if b == 1:
                    squares[t, s] = total
                else:
                    squares[t, s] = squares[t, s] + total

    def edge_stage(t, s):
        cur = lax.rem(t, 2)
        nxt = 1 - cur
        for side in range(2):

            @pl.when(has[side])
            def _():
                halo_copy(t, s, 1 - side).wait_recv()

            for i in range(HALO):
                x = i if side == 0 else slab - 1 - i
                sign = -1 if side == 0 else 1
                add = None
                for k in range(i + 1, HALO + 1):
                    term = REACH[k] * w[cur, s, low + x + sign * k]
                    add = term if add is None else add + term
                w[nxt, s, low + x] = w[nxt, s, low + x] + vel[x] * add

            @pl.when(has[side] & (t < steps - 1))
            def _():
                halo_copy(t + 1, s, side).start()

        for side in range(2):

            @pl.when(has[side])
            def _():
                halo_copy(t, s, side).wait_send()

        total = squares[t, s]
        for i in range(HALO):
            for x in (i, slab - 1 - i):
                total = total + record(t, s, x, w[nxt, s, low + x])
        squares[t, s] = total

        @pl.when(t == steps - 2)
        def _():
            before_copy(s).start()

        @pl.when(t == steps - 1)
        def _():
            last_copy(s).start()

    def before_copy(s):
        return pltpu.make_async_copy(
            w.at[(steps - 1) % 2, s, pl.ds(low, slab)], before_hbm.at[s], out_before.at[s]
        )

    def last_copy(s):
        return pltpu.make_async_copy(
            w.at[steps % 2, s, pl.ds(low, slab)], last_hbm.at[s], out_last.at[s]
        )

    rounds = 0
    while 2 ** (rounds + 1) < n // 2:
        rounds += 1
    rounds += 1

    def meet(m):
        for j in range(rounds + 1):

            @pl.when(m == shots + 1 + j)
            def _():
                if j > 0:
                    pl.semaphore_wait(ready_sem.at[j - 1], 2)
                if j < rounds:
                    for other in (lax.rem(me + 2**j, n), lax.rem(me + n - 2**j, n)):
                        pl.semaphore_signal(
                            ready_sem.at[j], inc=1, device_id={"gx": other}, device_id_type=MESH
                        )

    def turn(m, carry):
        s = lax.rem(m, shots)
        t = m // shots

        @pl.when(t > 0)
        def _():
            edge_stage(t - 1, s)

        @pl.when(t == 0)
        def _():
            mid_load(s).wait()
            prev_load(s).wait()

            @pl.when(s == 0)
            def _():
                for other in range(shots):
                    snap_load(other).wait()

        @pl.when(t < steps)
        def _():
            block_stage(t, s)

        meet(m)
        return carry

    lax.fori_loop(0, shots * (steps + 1), turn, 0)

    lane = lax.broadcasted_iota(jnp.int32, (1, 128), 1)
    mine = jnp.zeros((1, 128), F32)
    for t in range(steps):
        for s in range(shots):
            amount = jnp.sum(jnp.sum(squares[t, s], axis=0, keepdims=True), axis=1, keepdims=True)
            mine = jnp.where(lane == t * shots + s, amount, mine)
    row_mine[...] = mine
    partner = me + 1 - 2 * lax.rem(me, 2)
    pair = pltpu.make_async_remote_copy(
        src_ref=row_mine,
        dst_ref=row_partner,
        send_sem=pair_send,
        recv_sem=pair_recv,
        device_id={"gx": partner},
        device_id_type=MESH,
    )
    pair.start()
    pair.wait()
    chips = n // 2
    chip = me // 2
    both = mine + row_partner[...]
    row_chip[...] = both
    rows_all[chip] = both

    def share(k):
        return pltpu.make_async_remote_copy(
            src_ref=row_chip,
            dst_ref=rows_all.at[chip],
            send_sem=all_send,
            recv_sem=all_recv,
            device_id={"gx": lax.rem(me + 2 * k, n)},
            device_id_type=MESH,
        )

    for k in range(1, chips):
        share(k).start()
    everyone = pltpu.make_async_remote_copy(
        src_ref=rows_all.at[pl.ds(0, chips - 1)],
        dst_ref=rows_all.at[pl.ds(0, chips - 1)],
        send_sem=all_send,
        recv_sem=all_recv,
        device_id={"gx": right},
        device_id_type=MESH,
    )
    everyone.wait()
    energy = jnp.sum(rows_all[...], axis=0)
    cells = float(slab * ny * nz) * n
    weight = 1.0 / jnp.sqrt(energy / cells + 1e-6)

    weights = [weight[:, i : i + 1] for i in range(steps * shots)]

    def paint(x, carry):
        total = jnp.zeros((ny, nz), F32)
        for t in range(steps):
            for s in range(shots):
                total = total + weights[t * shots + s] * corr[t, s, x]
        image[x] = total
        image_copy(x).start()
        return carry

    def image_copy(x):
        return pltpu.make_async_copy(image.at[x], image_hbm.at[x], out_image.at[x])

    lax.fori_loop(0, slab, paint, 0)
    for t in range(steps):
        energy_out[t : t + 1, :] = energy[:, t * shots : (t + 1) * shots]
    for s in range(shots):
        before_copy(s).wait()
        last_copy(s).wait()
    for x in range(slab):
        image_copy(x).wait()


def per_device(
    n, now, prev, velocity, snapshots, traces, recv_x, recv_y, recv_z, recv_shot, snap_step
):
    shots, slab, ny, nz = now.shape
    snaps = snapshots.shape[1]
    steps, count = traces.shape
    blocks = slab // ROWS
    full = slab + 2 * HALO
    any_space = pl.BlockSpec(memory_space=pl.ANY)
    vmem = pl.BlockSpec(memory_space=pltpu.VMEM)
    smem = pl.BlockSpec(memory_space=pltpu.SMEM)
    dma = pltpu.SemaphoreType.DMA
    shape = functools.partial(jax.ShapeDtypeStruct, dtype=F32)
    return pl.pallas_call(
        functools.partial(kernel, n),
        out_shape=(
            shape((slab, ny, nz)),
            shape((shots, slab, ny, nz)),
            shape((shots, slab, ny, nz)),
            shape((steps, shots)),
        ),
        in_specs=[any_space] * 4 + [vmem] * 5 + [smem],
        out_specs=(any_space, any_space, any_space, vmem),
        scratch_shapes=[
            pltpu.VMEM((2, shots, full, ny, nz), F32),
            pltpu.VMEM((slab, ny, nz), F32),
            pltpu.VMEM((shots, snaps, slab, ny, nz), F32),
            pltpu.VMEM((steps, shots, slab, ny, nz), F32),
            pltpu.VMEM((shots * blocks, ROWS * ny, count), BF16),
            pltpu.VMEM((steps, 2, nz, count), BF16),
            pltpu.VMEM((ROWS * ny, ROWS * ny), BF16),
            pltpu.VMEM((nz, nz), BF16),
            pltpu.VMEM((steps, shots, 8, nz), F32),
            pltpu.VMEM((slab, ny, nz), F32),
            pltpu.VMEM((1, 128), F32),
            pltpu.VMEM((1, 128), F32),
            pltpu.VMEM((1, 128), F32),
            pltpu.VMEM((n // 2, 1, 128), F32),
            dma((2, shots)),
            dma((shots,)),
            dma((shots,)),
            dma,
            dma((shots,)),
            dma((2, steps, shots)),
            dma((2, steps, shots)),
            pltpu.SemaphoreType.REGULAR((8,)),
            dma,
            dma,
            dma,
            dma,
            dma((shots,)),
            dma((shots,)),
            dma((slab,)),
        ],
        compiler_params=pltpu.CompilerParams(
            collective_id=0, has_side_effects=True, vmem_limit_bytes=60 * 1024 * 1024
        ),
        name="rtm",
    )(
        now,
        prev,
        velocity,
        snapshots,
        traces,
        recv_x.reshape(1, -1),
        recv_y.reshape(1, -1),
        recv_z.reshape(1, -1),
        recv_shot.reshape(1, -1),
        snap_step,
    )


def solution(mesh):
    placed = (
        P("grp", "gx", None, None),
        P("grp", "gx", None, None),
        P(("grp", "gx"), None, None),
        P("grp", None, "gx", None, None),
        P("grp", None),
        P("grp"),
        P("grp"),
        P("grp"),
        P("grp"),
        P("grp", None),
    )
    return jax.shard_map(
        functools.partial(per_device, mesh.shape["gx"]),
        mesh=mesh,
        in_specs=placed,
        out_specs=(
            P(("grp", "gx"), None, None),
            P("grp", "gx", None, None),
            P("grp", "gx", None, None),
            P("grp", None),
        ),
        check_vma=False,
    )
```

time: 357 us -> 93 us (0.26)
  other arithmetic: 183 us -> 0 us
  local copies, waits for them, and re-layouts: 109 us -> 8.6 us
  Pallas kernels: 0 us -> 83.6 us
  starting transfers between devices: 47.3 us -> 0 us
  waiting for transfers between devices: 15.1 us -> 0 us
    reduce_sum x9 -> x0, other arithmetic: 84.7 us -> none  [the longest x4 77.2 us: record(): local = jnp.sum(fresh * fresh, axis=(1, 2, 3))]
    pallas_call x0 -> x1, Pallas kernels: none -> 83.6 us  [per_device(): pl.pallas_call(functools.partial(kernel, n), out_shape=(shape((slab, ny,...]
    add x3 -> x0, other arithmetic: 60.2 us -> none  [the longest x2 58.9 us: per_device(): 2.0 * now_wide[:, 4:-4] - prev_wide + speeds_wide[None] * laplace(now_wide)]
    gather x6 -> x0, local copies, waits for them, and re-layouts: 42.3 us -> none  [the longest x4 21.2 us: record(): chosen = snapshots[shot_ids, snap_step[step]]]
    unnamed x8 -> x0, other arithmetic: 38 us -> none
    ppermute x8 -> x0, starting transfers between devices: 29.1 us -> none  [the longest x4 17.6 us: padded_2(): lax.ppermute(lax.slice_in_dim(block, 0, width, axis=dim), axis, backward)]
    unnamed x61 -> x8, local copies, waits for them, and re-layouts: 35.9 us -> 8.6 us
    scatter-add x4 -> x0, local copies, waits for them, and re-layouts: 20.6 us -> none  [inject(): return field.at[recv_shot, place, recv_y, recv_z].add(source, mode='drop')]
  transfers between devices with their start and end apart: 9 -> 0, of which waited for: 2 -> 0; matrix products, arithmetic and copies ran while one was open for 15% -> 0% of each run, Pallas kernels for 0% -> 0%
where the time goes in v1:
time: 93 us; the launch traced here: 92.9 us
  Pallas kernels  83.6 us (90%)
  local copies, waits for them, and re-layouts  8.6 us (9%)
    pallas_call x1, Pallas kernels, per_device(): pl.pallas_call(functools.partial(kernel, n), out_shape=(shape((slab, ny,...  83.6 us
    unnamed x8, local copies, waits for them, and re-layouts  8.6 us

profile of v1, /device:TPU:69, one launch (start us, length us, event | category | flops | bytes accessed | tf_op | source)
XLA Modules:
  0.0 92.9 jit_solution(932601020932242408)
XLA Ops:
  0.6 83.6 %rtm.1 = (f32[16,64,256]{2,1,0:T(8,128)}, f32[3,16,64,256]{3,2,1,0:T(8,128)}, f32[3,16,64,256]{3,2,1,0:T(8,128)}, f32[4,3]{1,0:T(4,128)}) custom-call(f32[3,16,64,256]{3,2,1,0:T(8,128)} %now_hbm.1, f32[3,16,64,256]{3,2,1,0:T(8,128)} %prev_hbm.1, f32[16,64,256]{2,1,0:T(8,128)} %vel_hbm.1, f32[3,2,16,64,256]{4,3,2,1,0:T(8,128)} %snap_hbm.1, f32[4,1024]{1,0:T(4,128)} %traces.1, ...), custom_call_target="tpu_custom_call" | custom-call | tf_op jit(solution)/shard_map/rtm/pallas_call | solution.py:408
  84.2 2.3 %copy.18 = f32[16,64,256]{2,1,0:T(8,128)} copy(f32[16,64,256]{2,1,0:T(8,128)} %get-tuple-element.8) | data formatting | bytes 2097152
  86.5 0.0 copy-start
  86.5 4.1 %copy.19 = f32[3,16,64,256]{3,2,1,0:T(8,128)} copy(f32[3,16,64,256]{3,2,1,0:T(8,128)} %get-tuple-element.9) | data formatting | bytes 6291456
  90.6 0.0 copy-done
  90.6 0.0 copy-start.1
  90.6 1.7 %copy.20 = f32[3,16,64,256]{3,2,1,0:T(8,128)} copy(f32[3,16,64,256]{3,2,1,0:T(8,128)S(1)} %copy-done) | data formatting | bytes 6291456
  92.3 0.0 copy-done.1
  92.3 0.6 copy.21
Async XLA Ops:
  86.5 4.1 %copy-start = (f32[3,16,64,256]{3,2,1,0:T(8,128)S(1)}, f32[3,16,64,256]{3,2,1,0:T(8,128)}, u32[]{:S(2)}) copy-start(f32[3,16,64,256]{3,2,1,0:T(8,128)} %get-tuple-element.10) | copy-start | bytes 9437188
  90.6 1.7 %copy-start.1 = (f32[4,3]{1,0:T(4,128)S(1)}, f32[4,3]{1,0:T(4,128)}, u32[]{:S(2)}) copy-start(f32[4,3]{1,0:T(4,128)} %get-tuple-element.11) | copy-start | bytes 148

commit v2 on v1

--- a/solution.py
+++ b/solution.py
@@ -12,6 +12,9 @@
 CENTRE = -43050.0
 REACH = (0.0, 8064.0, -1008.0, 128.0, -9.0)
 HALO = 4
+FLIGHT = 64
+VMEM_SOURCES = 63 * 2**20
+VMEM_STEPS = 60 * 2**20
 ROWS = 4
 F32 = jnp.float32
 BF16 = jnp.bfloat16
@@ -38,26 +41,23 @@
     prev_hbm,
     vel_hbm,
     snap_hbm,
-    traces,
-    recv_x,
-    recv_y,
-    recv_z,
-    recv_shot,
+    sources_hbm,
     snap_step,
     image_hbm,
     last_hbm,
     before_hbm,
     energy_out,
-    w,
+    own,
+    image,
+    halo,
     vel,
     snap,
+    sources,
     corr,
-    onehot,
-    amps,
     band_y,
     band_z,
     squares,
-    image,
+    spread,
     row_mine,
     row_partner,
     row_chip,
@@ -67,6 +67,7 @@
     load_prev,
     load_vel,
     load_snap,
+    load_sources,
     send_sem,
     recv_sem,
     ready_sem,
@@ -79,9 +80,8 @@
     out_image,
 ):
     shots, slab, ny, nz = now_hbm.shape
-    steps, count = traces.shape
+    steps, snaps = sources_hbm.shape[0], snap_hbm.shape[1]
     blocks = slab // ROWS
-    low, high = HALO, HALO + slab
     me = lax.axis_index("gx")
     right, left = lax.rem(me + 1, n), lax.rem(me + n - 1, n)
 
@@ -90,23 +90,23 @@
         pl.semaphore_signal(barrier, inc=1, device_id={"gx": other}, device_id_type=MESH)
 
     def edge_load(s, side):
-        at = 0 if side == 0 else slab - HALO
+        planes = pl.ds(0 if side == 0 else slab - HALO, HALO)
         return pltpu.make_async_copy(
-            now_hbm.at[s, pl.ds(at, HALO)], w.at[0, s, pl.ds(low + at, HALO)], load_edge.at[side, s]
+            now_hbm.at[s, planes], own.at[0, s, planes], load_edge.at[side, s]
         )
 
     def mid_load(s):
-        return pltpu.make_async_copy(
-            now_hbm.at[s, pl.ds(HALO, slab - 2 * HALO)],
-            w.at[0, s, pl.ds(low + HALO, slab - 2 * HALO)],
-            load_mid.at[s],
-        )
+        planes = pl.ds(HALO, slab - 2 * HALO)
+        return pltpu.make_async_copy(now_hbm.at[s, planes], own.at[0, s, planes], load_mid.at[s])
 
     def prev_load(s):
-        return pltpu.make_async_copy(prev_hbm.at[s], w.at[1, s, pl.ds(low, slab)], load_prev.at[s])
+        return pltpu.make_async_copy(prev_hbm.at[s], own.at[1, s], load_prev.at[s])
 
     def snap_load(s):
         return pltpu.make_async_copy(snap_hbm.at[s], snap.at[s], load_snap.at[s])
+
+    def sources_load(t, s):
+        return pltpu.make_async_copy(sources_hbm.at[t, s], sources.at[t, s], load_sources.at[t, s])
 
     vel_load = pltpu.make_async_copy(vel_hbm, vel, load_vel)
 
@@ -117,18 +117,18 @@
     for s in range(shots):
         mid_load(s).start()
         prev_load(s).start()
-    for s in range(shots):
+        sources_load(0, s).start()
         snap_load(s).start()
+    for t in range(1, steps):
+        for s in range(shots):
+            sources_load(t, s).start()
 
     def halo_copy(t, s, side):
         parity = lax.rem(t, 2)
-        if side == 0:
-            source, target, device = low, high, left
-        else:
-            source, target, device = high - HALO, 0, right
+        device = left if side == 0 else right
         return pltpu.make_async_remote_copy(
-            src_ref=w.at[parity, s, pl.ds(source, HALO)],
-            dst_ref=w.at[parity, s, pl.ds(target, HALO)],
+            src_ref=own.at[parity, s, pl.ds(0 if side == 0 else slab - HALO, HALO)],
+            dst_ref=halo.at[parity, s, 1 - side],
             send_sem=send_sem.at[side, t, s],
             recv_sem=recv_sem.at[side, t, s],
             device_id={"gx": device},
@@ -147,33 +147,16 @@
                 halo_copy(0, s, side).start()
 
     zeros = jnp.zeros((HALO, ny, nz), F32)
-    for side, at in ((0, 0), (1, high)):
+    for side in range(2):
 
         @pl.when(jnp.logical_not(has[side]))
         def _():
             for parity in range(2):
                 for s in range(shots):
-                    w[parity, s, pl.ds(at, HALO)] = zeros
+                    halo[parity, s, side] = zeros
 
     band_y[...] = band(ROWS * ny, ny)
     band_z[...] = band(nz, nz)
-    local = recv_x[...] - me * slab
-    inside = (local >= 0) & (local < slab)
-    place = jnp.where(inside, (recv_shot[...] * slab + local) * ny + recv_y[...], -1)
-
-    def fill_onehot(b, carry):
-        index = lax.broadcasted_iota(jnp.int32, (ROWS * ny, count), 0) + b * (ROWS * ny)
-        onehot[b] = jnp.where(index == place, 1.0, 0.0).astype(BF16)
-        return carry
-
-    lax.fori_loop(0, shots * blocks, fill_onehot, 0)
-    along = lax.broadcasted_iota(jnp.int32, (nz, count), 0) == recv_z[...]
-    for t in range(steps):
-        amp = traces[t : t + 1, :] * SCALE
-        top = amp.astype(BF16).astype(F32)
-        amps[t, 0] = jnp.where(along, top, 0.0).astype(BF16)
-        amps[t, 1] = jnp.where(along, amp - top, 0.0).astype(BF16)
-
     vel_load.wait()
     vel[...] = vel[...] * (1.0 / SCALE)
 
@@ -181,7 +164,9 @@
         return jnp.sum(value.reshape(ny // 8, 8, nz), axis=0)
 
     def record(t, s, x, fresh):
-        chosen = snap[s, snap_step[t, s], x]
+        chosen = snap[s, 0, x]
+        for k in range(1, snaps):
+            chosen = jnp.where(snap_step[t, s] == k, snap[s, k, x], chosen)
         corr[t, s, x] = chosen * fresh
         return fold(fresh * fresh)
 
@@ -191,29 +176,23 @@
         for b in range(blocks):
             inner = 0 < b < blocks - 1
             x0 = b * ROWS
-            v = w[cur, s, pl.ds(low + x0, ROWS)].reshape(ROWS * ny, nz)
+            v = own[cur, s, pl.ds(x0, ROWS)].reshape(ROWS * ny, nz)
             top = v.astype(BF16)
             rest = (v - top.astype(F32)).astype(BF16)
             acc = dot(top, band_z[...]) + dot(rest, band_z[...])
             acc = acc + dot(band_y[...], top) + dot(band_y[...], rest)
-            hot = onehot[s * blocks + b]
-            acc = acc + dot(hot, amps[t, 0], ((1,), (1,))) + dot(hot, amps[t, 1], ((1,), (1,)))
             acc = acc.reshape(ROWS, ny, nz)
             total = jnp.zeros((8, nz), F32)
             for i in range(ROWS):
                 x = x0 + i
-                centre = w[cur, s, low + x]
-                value = acc[i] + CENTRE * centre
+                centre = own[cur, s, x]
+                value = acc[i] + sources[t, s, x] + CENTRE * centre
                 for k in range(1, HALO + 1):
-                    near = []
-                    if x + k < slab:
-                        near.append(w[cur, s, low + x + k])
-                    if x - k >= 0:
-                        near.append(w[cur, s, low + x - k])
+                    near = [own[cur, s, y] for y in (x + k, x - k) if 0 <= y < slab]
                     pair = near[0] + near[1] if len(near) == 2 else near[0]
                     value = value + REACH[k] * pair
-                fresh = 2.0 * centre - w[nxt, s, low + x] + vel[x] * value
-                w[nxt, s, low + x] = fresh
+                fresh = 2.0 * centre - own[nxt, s, x] + vel[x] * value
+                own[nxt, s, x] = fresh
                 if inner:
                     total = total + record(t, s, x, fresh)
             if inner:
@@ -233,12 +212,13 @@
 
             for i in range(HALO):
                 x = i if side == 0 else slab - 1 - i
-                sign = -1 if side == 0 else 1
                 add = None
                 for k in range(i + 1, HALO + 1):
-                    term = REACH[k] * w[cur, s, low + x + sign * k]
+                    far = k - i - 1
+                    plane = halo[cur, s, side, HALO - 1 - far if side == 0 else far]
+                    term = REACH[k] * plane
                     add = term if add is None else add + term
-                w[nxt, s, low + x] = w[nxt, s, low + x] + vel[x] * add
+                own[nxt, s, x] = own[nxt, s, x] + vel[x] * add
 
             @pl.when(has[side] & (t < steps - 1))
             def _():
@@ -253,7 +233,7 @@
         total = squares[t, s]
         for i in range(HALO):
             for x in (i, slab - 1 - i):
-                total = total + record(t, s, x, w[nxt, s, low + x])
+                total = total + record(t, s, x, own[nxt, s, x])
         squares[t, s] = total
 
         @pl.when(t == steps - 2)
@@ -266,13 +246,11 @@
 
     def before_copy(s):
         return pltpu.make_async_copy(
-            w.at[(steps - 1) % 2, s, pl.ds(low, slab)], before_hbm.at[s], out_before.at[s]
+            own.at[(steps - 1) % 2, s], before_hbm.at[s], out_before.at[s]
         )
 
     def last_copy(s):
-        return pltpu.make_async_copy(
-            w.at[steps % 2, s, pl.ds(low, slab)], last_hbm.at[s], out_last.at[s]
-        )
+        return pltpu.make_async_copy(own.at[steps % 2, s], last_hbm.at[s], out_last.at[s])
 
     rounds = 0
     while 2 ** (rounds + 1) < n // 2:
@@ -304,14 +282,11 @@
         def _():
             mid_load(s).wait()
             prev_load(s).wait()
-
-            @pl.when(s == 0)
-            def _():
-                for other in range(shots):
-                    snap_load(other).wait()
+            snap_load(s).wait()
 
         @pl.when(t < steps)
         def _():
+            sources_load(t, s).wait()
             block_stage(t, s)
 
         meet(m)
@@ -367,15 +342,17 @@
     energy = jnp.sum(rows_all[...], axis=0)
     cells = float(slab * ny * nz) * n
     weight = 1.0 / jnp.sqrt(energy / cells + 1e-6)
-
-    weights = [weight[:, i : i + 1] for i in range(steps * shots)]
-
+    for i in range(steps * shots):
+        spread[i] = jnp.broadcast_to(weight[:, i : i + 1], (8, 128))
     def paint(x, carry):
-        total = jnp.zeros((ny, nz), F32)
-        for t in range(steps):
-            for s in range(shots):
-                total = total + weights[t * shots + s] * corr[t, s, x]
-        image[x] = total
+        for y in range(0, ny, 8):
+            for z in range(0, nz, 128):
+                total = None
+                for t in range(steps):
+                    for s in range(shots):
+                        part = corr[t, s, x, y : y + 8, z : z + 128] * spread[t * shots + s]
+                        total = part if total is None else total + part
+                image[x, y : y + 8, z : z + 128] = total
         image_copy(x).start()
         return carry
 
@@ -392,19 +369,153 @@
         image_copy(x).wait()
 
 
+def gather_sources(
+    traces_hbm,
+    x_hbm,
+    y_hbm,
+    z_hbm,
+    shot_hbm,
+    out,
+    dense,
+    blank,
+    traces,
+    recv_x,
+    recv_y,
+    recv_z,
+    recv_shot,
+    found,
+    load_sem,
+    blank_sem,
+    tile_sem,
+):
+    steps, shots, slab, ny, nz = out.shape
+    count = traces.shape[1]
+    pairs = (
+        (x_hbm, recv_x),
+        (traces_hbm, traces),
+        (y_hbm, recv_y),
+        (z_hbm, recv_z),
+        (shot_hbm, recv_shot),
+    )
+    loads = [pltpu.make_async_copy(a, b, load_sem.at[i]) for i, (a, b) in enumerate(pairs)]
+    for load in loads:
+        load.start()
+    start = lax.axis_index("gx") * slab
+    zeros = jnp.zeros((ny, nz), F32)
+
+    def clear_blank(x, carry):
+        blank[x] = zeros
+        return carry
+
+    lax.fori_loop(0, slab, clear_blank, 0)
+
+    def blank_copy(t, s):
+        return pltpu.make_async_copy(blank, out.at[t, s], blank_sem.at[t, s])
+
+    for t in range(steps):
+        for s in range(shots):
+            blank_copy(t, s).start()
+
+    def clear(x, carry):
+        for t in range(steps):
+            for s in range(shots):
+                dense[t, s, x] = zeros
+        return carry
+
+    lax.fori_loop(0, slab, clear, 0)
+    for load in loads:
+        load.wait()
+
+    group = 16
+
+    def scan(i, total):
+        for j in range(group):
+            r = i * group + j
+            local = recv_x[r] - start
+            found[total] = r
+            inside = (local >= 0) & (local < slab)
+            total = total + inside.astype(jnp.int32)
+        return total
+
+    total = lax.fori_loop(0, count // group, scan, 0)
+    lane = lax.broadcasted_iota(jnp.int32, (1, nz), 1)
+
+    def add(i, carry):
+        r = found[i]
+        s, x, y = recv_shot[r], recv_x[r] - start, recv_y[r]
+        here = lane == recv_z[r]
+        for t in range(steps):
+            row = dense[t, s, x, pl.ds(y, 1), :]
+            dense[t, s, x, pl.ds(y, 1), :] = row + jnp.where(here, traces[t, r] * SCALE, 0.0)
+        return carry
+
+    lax.fori_loop(0, total, add, 0)
+    for t in range(steps):
+        for s in range(shots):
+            blank_copy(t, s).wait()
+
+    def tile_copy(i, t):
+        r = found[i]
+        s, x = recv_shot[r], recv_x[r] - start
+        rows = pl.ds(pl.multiple_of((recv_y[r] // 8) * 8, 8), 8)
+        return pltpu.make_async_copy(
+            dense.at[t, s, x, rows], out.at[t, s, x, rows], tile_sem.at[lax.rem(i, FLIGHT), t]
+        )
+
+    def chunk(c, carry):
+        first = c * FLIGHT
+        last = jnp.minimum(first + FLIGHT, total)
+
+        def begin(i, carry):
+            for t in range(steps):
+                tile_copy(i, t).start()
+            return carry
+
+        def finish(i, carry):
+            for t in range(steps):
+                tile_copy(i, t).wait()
+            return carry
+
+        lax.fori_loop(first, last, begin, 0)
+        lax.fori_loop(first, last, finish, 0)
+        return carry
+
+    lax.fori_loop(0, (total + FLIGHT - 1) // FLIGHT, chunk, 0)
+
+
 def per_device(
     n, now, prev, velocity, snapshots, traces, recv_x, recv_y, recv_z, recv_shot, snap_step
 ):
     shots, slab, ny, nz = now.shape
     snaps = snapshots.shape[1]
     steps, count = traces.shape
-    blocks = slab // ROWS
-    full = slab + 2 * HALO
-    any_space = pl.BlockSpec(memory_space=pl.ANY)
+    hbm = pl.BlockSpec(memory_space=pltpu.HBM)
     vmem = pl.BlockSpec(memory_space=pltpu.VMEM)
     smem = pl.BlockSpec(memory_space=pltpu.SMEM)
     dma = pltpu.SemaphoreType.DMA
     shape = functools.partial(jax.ShapeDtypeStruct, dtype=F32)
+    ints = pltpu.SMEM((count,), jnp.int32)
+    sources = pl.pallas_call(
+        gather_sources,
+        out_shape=shape((steps, shots, slab, ny, nz)),
+        in_specs=[hbm] * 5,
+        out_specs=hbm,
+        scratch_shapes=[
+            pltpu.VMEM((steps, shots, slab, ny, nz), F32),
+            pltpu.VMEM((slab, ny, nz), F32),
+            pltpu.SMEM((steps, count), F32),
+            ints,
+            ints,
+            ints,
+            ints,
+            pltpu.SMEM((count + 1,), jnp.int32),
+            dma((5,)),
+            dma((steps, shots)),
+            dma((FLIGHT, steps)),
+        ],
+        compiler_params=pltpu.CompilerParams(vmem_limit_bytes=VMEM_SOURCES),
+        name="sources",
+    )(traces, recv_x, recv_y, recv_z, recv_shot)
     return pl.pallas_call(
         functools.partial(kernel, n),
         out_shape=(
@@ -413,19 +524,20 @@
             shape((shots, slab, ny, nz)),
             shape((steps, shots)),
         ),
-        in_specs=[any_space] * 4 + [vmem] * 5 + [smem],
-        out_specs=(any_space, any_space, any_space, vmem),
+        in_specs=[hbm] * 5 + [smem],
+        out_specs=(hbm, hbm, hbm, vmem),
         scratch_shapes=[
-            pltpu.VMEM((2, shots, full, ny, nz), F32),
+            pltpu.VMEM((2, shots, slab, ny, nz), F32),
+            pltpu.VMEM((slab, ny, nz), F32),
+            pltpu.VMEM((2, shots, 2, HALO, ny, nz), F32),
             pltpu.VMEM((slab, ny, nz), F32),
             pltpu.VMEM((shots, snaps, slab, ny, nz), F32),
             pltpu.VMEM((steps, shots, slab, ny, nz), F32),
-            pltpu.VMEM((shots * blocks, ROWS * ny, count), BF16),
-            pltpu.VMEM((steps, 2, nz, count), BF16),
+            pltpu.VMEM((steps, shots, slab, ny, nz), F32),
             pltpu.VMEM((ROWS * ny, ROWS * ny), BF16),
             pltpu.VMEM((nz, nz), BF16),
             pltpu.VMEM((steps, shots, 8, nz), F32),
-            pltpu.VMEM((slab, ny, nz), F32),
+            pltpu.VMEM((steps * shots, 8, 128), F32),
             pltpu.VMEM((1, 128), F32),
             pltpu.VMEM((1, 128), F32),
             pltpu.VMEM((1, 128), F32),
@@ -435,6 +547,7 @@
             dma((shots,)),
             dma,
             dma((shots,)),
+            dma((steps, shots)),
             dma((2, steps, shots)),
             dma((2, steps, shots)),
             pltpu.SemaphoreType.REGULAR((8,)),
@@ -447,21 +560,10 @@
             dma((slab,)),
         ],
         compiler_params=pltpu.CompilerParams(
-            collective_id=0, has_side_effects=True, vmem_limit_bytes=60 * 1024 * 1024
+            collective_id=0, has_side_effects=True, vmem_limit_bytes=VMEM_STEPS
         ),
         name="rtm",
-    )(
-        now,
-        prev,
-        velocity,
-        snapshots,
-        traces,
-        recv_x.reshape(1, -1),
-        recv_y.reshape(1, -1),
-        recv_z.reshape(1, -1),
-        recv_shot.reshape(1, -1),
-        snap_step,
-    )
+    )(now, prev, velocity, snapshots, sources, snap_step)
 
 
 def solution(mesh):

time: 93 us -> 83.2 us (0.89)
  Pallas kernels: 83.6 us -> 73.8 us
    pallas_call x1, Pallas kernels: 83.6 us -> 64.5 us  [per_device(): pl.pallas_call(functools.partial(kernel, n), out_shape=(shape((slab, ny,...]
    pallas_call x0 -> x1, Pallas kernels: none -> 9.33 us  [per_device(): pl.pallas_call(gather_sources, out_shape=shape((steps, shots, slab, ny, n...]
where the time goes in v2:
time: 83.2 us; the launch traced here: 83 us
  Pallas kernels  73.8 us (89%)
  local copies, waits for them, and re-layouts  8.6 us (10%)
    pallas_call x1, Pallas kernels, per_device(): pl.pallas_call(functools.partial(kernel, n), out_shape=(shape((slab, ny,...  64.5 us
    pallas_call x1, Pallas kernels, per_device(): pl.pallas_call(gather_sources, out_shape=shape((steps, shots, slab, ny, n...  9.33 us
    unnamed x8, local copies, waits for them, and re-layouts  8.6 us

profile of v2, /device:TPU:69, one launch (start us, length us, event | category | flops | bytes accessed | tf_op | source)
XLA Modules:
  0.0 83.0 jit_solution(913242846804487069)
XLA Ops:
  0.6 9.3 %sources.1.sources_hbm = f32[4,3,16,64,256]{4,3,2,1,0:T(8,128)} custom-call(f32[4,1024]{1,0:T(4,128)} %traces_hbm.1, s32[1024]{0:T(1024)} %x_hbm.1, s32[1024]{0:T(1024)} %y_hbm.1, s32[1024]{0:T(1024)} %z_hbm.1, s32[1024]{0:T(1024)} %shot_hbm.1), custom_call_target="tpu_custom_call" | custom-call | tf_op jit(solution)/shard_map/sources/pallas_call | solution.py:498
  10.0 64.5 %rtm.1 = (f32[16,64,256]{2,1,0:T(8,128)}, f32[3,16,64,256]{3,2,1,0:T(8,128)}, f32[3,16,64,256]{3,2,1,0:T(8,128)}, f32[4,3]{1,0:T(4,128)}) custom-call(f32[3,16,64,256]{3,2,1,0:T(8,128)} %now_hbm.1, f32[3,16,64,256]{3,2,1,0:T(8,128)} %prev_hbm.1, f32[16,64,256]{2,1,0:T(8,128)} %vel_hbm.1, f32[3,2,16,64,256]{4,3,2,1,0:T(8,128)} %snap_hbm.1, ...), custom_call_target="tpu_custom_call" | custom-call | tf_op jit(solution)/shard_map/rtm/pallas_call | solution.py:519
  74.4 2.3 %copy.18 = f32[16,64,256]{2,1,0:T(8,128)} copy(f32[16,64,256]{2,1,0:T(8,128)} %get-tuple-element.8) | data formatting | bytes 2097152
  76.7 0.0 copy-start
  76.7 4.1 %copy.19 = f32[3,16,64,256]{3,2,1,0:T(8,128)} copy(f32[3,16,64,256]{3,2,1,0:T(8,128)} %get-tuple-element.9) | data formatting | bytes 6291456
  80.8 0.0 copy-done
  80.8 0.0 copy-start.1
  80.8 1.7 %copy.20 = f32[3,16,64,256]{3,2,1,0:T(8,128)} copy(f32[3,16,64,256]{3,2,1,0:T(8,128)S(1)} %copy-done) | data formatting | bytes 6291456
  82.5 0.0 copy-done.1
  82.5 0.6 copy.21
Async XLA Ops:
  76.7 4.1 %copy-start = (f32[3,16,64,256]{3,2,1,0:T(8,128)S(1)}, f32[3,16,64,256]{3,2,1,0:T(8,128)}, u32[]{:S(2)}) copy-start(f32[3,16,64,256]{3,2,1,0:T(8,128)} %get-tuple-element.10) | copy-start | bytes 9437188
  80.8 1.7 %copy-start.1 = (f32[4,3]{1,0:T(4,128)S(1)}, f32[4,3]{1,0:T(4,128)}, u32[]{:S(2)}) copy-start(f32[4,3]{1,0:T(4,128)} %get-tuple-element.11) | copy-start | bytes 148
